TPU v7x, 32 devices: a whole 2x2x4 slice. The times are simulated.
32 devices in a mesh: expert: 4 (over y, x), tensor: 4 (over z), rep: 2 (over core).
Axes of the slice: x: 2, y: 2, z: 4, core: 2. Of those that a mesh axis runs over, the one named last changes fastest.
Arguments:
- requests: bfloat16 [512, 1536], P('expert', ('tensor', 'rep')), may hold values from -6 to 6
- expert_ids: int32 [512, 2], P('expert'), may hold values from 0 to 3, all different within a row; in each aligned block of 128 rows (0 to 127, 128 to 255, ...) at most 96 rows name the same one
- gate_values: float32 [512, 2], P('expert'), may hold values from 0.2 to 1
- w_up: bfloat16 [4, 1536, 6144], P(None, 'expert', ('tensor', 'rep')), may hold values from -0.15625 to 0.15625
- w_down: bfloat16 [4, 1536, 6144], P(None, 'expert', ('tensor', 'rep')), may hold values from -0.078125 to 0.078125
- tower_in: bfloat16 [1536, 768], P(('tensor', 'rep')), may hold values from -0.15625 to 0.15625
- tower_bias: float32 [768], replicated, may hold values from -3 to 3
- tower_out: float32 [3, 256], replicated, may hold values from -0.375 to 0.375
- out_bias: float32 [3], replicated, may hold values from -3 to 3
Outputs:
- mixed: bfloat16 [512, 1536], P('expert', ('tensor', 'rep'))
- scores: float32 [3, 512], P(None, ('expert', 'tensor', 'rep'))
Inputs may be any that keep to these rules, and one draw needn't show every extreme that they name: `expert_ids`: each row names two different experts. In the rows of one device (128 requests) no expert is named more than 96 times, a bound that some block reaches.
All inputs are finite; a program needn't handle non-finite values.
Results may differ from a plain program's by a relative error of at most 0.015.
Values may be sent and summed in bfloat16 or wider, within the bound.
No kernel may reach another device: no remote copies, remote signals or barrier semaphores. Data moves between devices by JAX's collectives and lax.ppermute only.
A program may use at most 64 MiB of HBM per device.

v0:
```python
import jax
import jax.numpy as jnp
from jax import lax
from jax.sharding import PartitionSpec as P


def tower_head(pre, tower_bias, tower_out, out_bias):
    active = jax.nn.relu(pre + tower_bias[None, :])
    active = active.reshape(pre.shape[0], tower_out.shape[0], tower_out.shape[1])
    logits = jnp.sum(active * tower_out[None, :, :], axis=2) + out_bias[None, :]
    return jax.nn.sigmoid(logits).T


def per_device(
    requests, expert_ids, gate_values, w_up, w_down, tower_in, tower_bias, tower_out, out_bias
):
    groups = lax.axis_size("expert")
    experts = w_up.shape[0]
    local_experts = experts // groups
    tok_rows = requests.shape[0]
    capacity = 3 * tok_rows // experts
    serve_up, serve_down = (
        lax.all_to_all(w_up, "expert", split_axis=0, concat_axis=1, tiled=True),
        lax.all_to_all(w_down, "expert", split_axis=0, concat_axis=1, tiled=True),
    )
    flat_ids = expert_ids.reshape(-1)
    onehot = (flat_ids[:, None] == jnp.arange(experts, dtype=jnp.int32)[None, :]).astype(jnp.int32)
    before = jnp.cumsum(onehot, axis=0) - onehot
    slot_rank = jnp.sum(before * onehot, axis=1)
    slots = (flat_ids * capacity + slot_rank).reshape(tok_rows, 2)
    slot_index = jnp.arange(experts * capacity, dtype=jnp.int32)
    spread = (
        (slot_index[:, None] == slots[None, :, 0]) | (slot_index[:, None] == slots[None, :, 1])
    ).astype(jnp.bfloat16)
    full_rows = lax.all_gather(requests, ("tensor", "rep"), axis=1, tiled=True)
    outgoing = jnp.dot(spread, full_rows, preferred_element_type=jnp.float32).astype(jnp.bfloat16)
    incoming = lax.all_to_all(outgoing, "expert", split_axis=0, concat_axis=0, tiled=True)
    shaped = incoming.reshape(groups, local_experts, capacity, incoming.shape[1])
    hidden_pre = jnp.einsum("secd,edh->sech", shaped, serve_up, preferred_element_type=jnp.float32)
    hidden = jax.nn.relu(hidden_pre).astype(jnp.bfloat16)
    partial_value = jnp.einsum(
        "sech,edh->secd", hidden, serve_down, preferred_element_type=jnp.float32
    )
    summed = lax.psum_scatter(
        partial_value.astype(jnp.bfloat16), ("tensor", "rep"), scatter_dimension=3, tiled=True
    ).astype(jnp.float32)
    expert_out = summed.astype(jnp.bfloat16).reshape(
        groups * local_experts * capacity, summed.shape[3]
    )
    returned = lax.all_to_all(expert_out, "expert", split_axis=0, concat_axis=0, tiled=True)
    pick_first = (slots[:, 0:1] == slot_index[None, :]).astype(jnp.bfloat16)
    pick_second = (slots[:, 1:2] == slot_index[None, :]).astype(jnp.bfloat16)
    first = jnp.dot(pick_first, returned, preferred_element_type=jnp.float32)
    second = jnp.dot(pick_second, returned, preferred_element_type=jnp.float32)
    mixed = (gate_values[:, 0:1] * first + gate_values[:, 1:2] * second).astype(jnp.bfloat16)
    pre = lax.psum_scatter(
        jnp.dot(mixed, tower_in, preferred_element_type=jnp.float32).astype(jnp.bfloat16),
        ("tensor", "rep"),
        scatter_dimension=0,
        tiled=True,
    ).astype(jnp.float32)
    scores = tower_head(pre, tower_bias, tower_out, out_bias)
    return (mixed, scores)


def solution(mesh):
    in_specs = (
        P("expert", ("tensor", "rep")),
        P("expert", None),
        P("expert", None),
        P(None, "expert", ("tensor", "rep")),
        P(None, "expert", ("tensor", "rep")),
        P(("tensor", "rep"), None),
        P(),
        P(),
        P(),
    )
    out_specs = (P("expert", ("tensor", "rep")), P(None, ("expert", "tensor", "rep")))
    return jax.shard_map(
        per_device, mesh=mesh, in_specs=in_specs, out_specs=out_specs, check_vma=False
    )
```

profile of v0, /device:TPU:0, one launch (start us, length us, event | category | flops | bytes accessed | tf_op | source)
XLA Modules:
  0.0 198.6 jit_solution(8744839714044765721)
XLA Ops:
  7.2 0.0 copy-start
  7.2 0.0 reduce-scatter.7.cloned.1.call-start
  7.2 0.8 copy.32
  8.0 0.1 eq.85
  8.2 0.1 eq.81
  8.3 1.2 reduce-window.6
  9.6 0.1 slice.26
  9.6 0.1 copy.34
  9.8 0.1 copy.35
  9.9 0.1 add_bitcast_fusion
  10.0 0.1 reduce_sum.21
  10.1 0.1 copy.36
  10.2 0.7 multiply_add_fusion
  10.9 16.4 %all_gather.3 = bf16[128,1536]{0,1:T(8,128)(2,1)S(1)} all-gather(bf16[128,192]{0,1:T(8,128)(2,1)} %param.9), channel_id=1, replica_groups=mesh['expert'=4,'tensor'=4,'rep'=2] {'tensor','rep'}, dimensions={1}, use_global_device_ids=true | all-gather | bytes 442368 | tf_op jit(solution)/shard_map/all_gather | solution.py:35
  27.3 0.5 convolution_convert_fusion
  27.8 0.0 copy-start.1
  27.8 19.8 %all_to_all.39 = bf16[4,96,1536]{2,1,0:T(8,128)(2,1)} all-to-all(bf16[4,96,1536]{2,1,0:T(8,128)(2,1)S(1)} %bitcast.56), channel_id=1, replica_groups=mesh['expert'=4,'tensor'=4,'rep'=2] {'expert'}, dimensions={0} | all-to-all | bytes 2359296 | tf_op jit(solution)/shard_map/all_to_all | solution.py:37
  47.6 0.0 copy-done.1
  47.6 30.1 %all_to_all.40 = bf16[4,384,768]{2,1,0:T(8,128)(2,1)S(1)} all-to-all(bf16[4,384,768]{2,1,0:T(8,128)(2,1)S(1)} %copy-done.1), channel_id=1, replica_groups=mesh['expert'=4,'tensor'=4,'rep'=2] {'expert'}, dimensions={0} | all-to-all | bytes 4718592 | tf_op jit(solution)/shard_map/all_to_all | solution.py:23
  77.7 0.0 copy-done.2
  77.7 29.5 %all_to_all.41 = bf16[4,384,768]{2,1,0:T(8,128)(2,1)} all-to-all(bf16[4,384,768]{2,1,0:T(8,128)(2,1)S(1)} %copy-done.2), channel_id=1, replica_groups=mesh['expert'=4,'tensor'=4,'rep'=2] {'expert'}, dimensions={0} | all-to-all | bytes 4718592 | tf_op jit(solution)/shard_map/all_to_all | solution.py:24
  107.3 5.5 %fusion = bf16[4,1,96,1536]{3,2,0,1:T(8,128)(2,1)} fusion(bf16[1536,768,1]{1,0,2:T(8,128)(2,1)} %bitcast.58, bf16[4,96,1536]{2,1,0:T(8,128)(2,1)} %all_to_all.39, bf16[1536,768,1]{1,0,2:T(8,128)(2,1)S(1)} %bitcast.57), kind=kOutput, calls=%fused_computation.2 | convolution fusion | flops 1813118976 | bytes 7077888 | tf_op jit(solution)/shard_map/sech,edh->secd/dot_general | solution.py:41
  112.7 2.6 %copy.38 = bf16[4,1,96,1536]{2,0,1,3:T(4,128)(2,1)S(1)} copy(bf16[4,1,96,1536]{3,2,0,1:T(8,128)(2,1)} %fusion) | data formatting | bytes 2359296
  115.4 1.9 reshape.69
  117.3 0.0 reduce-scatter.7.cloned.1.call-update
  117.3 0.0 copy-start.5
  117.3 0.0 copy-start.7
  117.3 32.7 %reduce-scatter.7.cloned.1.call-done = bf16[192,384]{1,0:T(8,128)(2,1)} async-done(((bf16[1536,384]{1,0:T(8,128)(2,1)}), bf16[192,384]{1,0:T(8,128)(2,1)}) %reduce-scatter.7.cloned.1.call-update) | async-done | bytes 147472
  150.0 1.1 reshape.70
  151.0 0.8 copy.39
  151.9 3.6 %all-to-all-start.3 = ((bf16[4,96,192]{2,1,0:T(8,128)(2,1)}), bf16[4,96,192]{2,1,0:T(8,128)(2,1)S(1)}, u32[]{:S(2)}, u32[]{:S(2)}) async-start(bf16[4,96,192]{2,1,0:T(8,128)(2,1)} %bitcast.13), calls=%async_computation.3 | async-start | bytes 393216 | tf_op jit(solution)/shard_map/all_to_all | solution.py:50
  155.5 0.0 reduce-scatter.5.cloned.1.call-start
  155.5 0.0 copy-done.6
  155.5 5.2 %all-to-all-done.3 = bf16[4,96,192]{2,1,0:T(8,128)(2,1)S(1)} async-done(((bf16[4,96,192]{2,1,0:T(8,128)(2,1)}), bf16[4,96,192]{2,1,0:T(8,128)(2,1)S(1)}, u32[]{:S(2)}, u32[]{:S(2)}) %all-to-all-start.3) | async-done | bytes 147488 | tf_op jit(solution)/shard_map/all_to_all | solution.py:50
  160.7 0.3 convolution_multiply_fusion
  161.0 0.3 fusion.3
  161.3 0.0 copy-done
  161.3 0.0 copy-start.3
  161.3 0.9 convolution_convert_fusion.2
  162.2 0.0 reduce-scatter.5.cloned.1.call-update
  162.2 27.9 %reduce-scatter.5.cloned.1.call-done = bf16[16,768]{1,0:T(8,128)(2,1)} async-done(((bf16[128,768]{1,0:T(8,128)(2,1)}), bf16[16,768]{1,0:T(8,128)(2,1)}) %reduce-scatter.5.cloned.1.call-update) | async-done | bytes 24592 | tf_op jit(solution)/shard_map/reduce_scatter | solution.py:56
  190.2 0.0 copy-done.4
  190.2 0.7 add_maximum_fusion
  190.9 0.0 copy-done.5
  191.0 0.1 multiply_reduce_fusion
  191.1 0.0 copy-done.7
  191.1 0.7 copy.37
  191.7 0.0 copy-done.3
  (11 shorter events, 0.1 us)
Async XLA Ops:
  7.2 154.1 %copy-start = (bf16[192,768]{1,0:T(8,128)(2,1)S(1)}, bf16[192,768]{1,0:T(8,128)(2,1)}, u32[]{:S(2)}) copy-start(bf16[192,768]{1,0:T(8,128)(2,1)} %param.14) | copy-start | bytes 884740
  7.2 142.8 %reduce-scatter.7.cloned.1.call-start = ((), (), s32[]{:S(2)}) async-start(), calls=%async_computation.7 | async-start | bytes 1327104
  27.8 19.8 %copy-start.1 = (bf16[4,384,768]{2,1,0:T(8,128)(2,1)S(1)}, bf16[4,384,768]{2,1,0:T(8,128)(2,1)}, u32[]{:S(2)}) copy-start(bf16[4,384,768]{2,1,0:T(8,128)(2,1)} %param.12) | copy-start | bytes 7077892
  47.6 30.1 %copy-start.2 = (bf16[4,384,768]{2,1,0:T(8,128)(2,1)S(1)}, bf16[4,384,768]{2,1,0:T(8,128)(2,1)}, u32[]{:S(2)}) copy-start(bf16[4,384,768]{2,1,0:T(8,128)(2,1)} %param.13) | copy-start | bytes 7077892
  117.3 38.2 %copy-start.6 = (f32[128,2]{0,1:T(2,128)S(1)}, f32[128,2]{0,1:T(2,128)}, u32[]{:S(2)}) copy-start(f32[128,2]{0,1:T(2,128)} %param.11) | copy-start | bytes 3076
  117.3 72.9 %copy-start.4 = (f32[768]{0:T(1024)S(1)}, f32[768]{0:T(1024)}, u32[]{:S(2)}) copy-start(f32[768]{0:T(1024)} %param.15) | copy-start | bytes 9220
  117.3 73.7 %copy-start.5 = (f32[3,256]{1,0:T(4,128)S(1)}, f32[3,256]{1,0:T(4,128)}, u32[]{:S(2)}) copy-start(f32[3,256]{1,0:T(4,128)} %param.16) | copy-start | bytes 9220
  117.3 73.7 %copy-start.7 = (f32[3]{0:T(128)S(1)}, f32[3]{0:T(128)}, u32[]{:S(2)}) copy-start(f32[3]{0:T(128)} %param.17) | copy-start | bytes 40
  151.9 8.8 %all-to-all-start.3 = ((bf16[4,96,192]{2,1,0:T(8,128)(2,1)}), bf16[4,96,192]{2,1,0:T(8,128)(2,1)S(1)}, u32[]{:S(2)}, u32[]{:S(2)}) async-start(bf16[4,96,192]{2,1,0:T(8,128)(2,1)} %bitcast.13), calls=%async_computation.3 | async-start | bytes 393216 | tf_op jit(solution)/shard_map/all_to_all | solution.py:50
  155.5 34.7 %reduce-scatter.5.cloned.1.call-start = ((), (), s32[]{:S(2)}) async-start(), calls=%async_computation.6 | async-start | bytes 221184 | tf_op jit(solution)/shard_map/reduce_scatter | solution.py:56
  161.3 30.5 %copy-start.3 = (bf16[128,192]{0,1:T(8,128)(2,1)}, bf16[128,192]{0,1:T(8,128)(2,1)S(1)}, u32[]{:S(2)}) copy-start(bf16[128,192]{0,1:T(8,128)(2,1)S(1)} %fusion.3) | copy-start | bytes 147460
Sparse Core Ops, SparseCore 0:
  117.4 32.5 reduce-scatter.6
  162.4 27.7 reduce-scatter.4
where the time goes:
time: 199 us
  blocking collectives  95.8 us (48%)
  waiting for transfers between devices  65.8 us (33%)
  between operations  14.2 us (7%)
  local copies, waits for them, and re-layouts  8.73 us (4%)
  matrix products  7.42 us (4%)
  starting transfers between devices  3.68 us (2%)
  other arithmetic  2.92 us (1%)
    unnamed x3, waiting for transfers between devices  32.7 us
    all_to_all x1, blocking collectives, per_device(): lax.all_to_all(w_up, 'expert', split_axis=0, concat_axis=1, tiled=True)  30.1 us
    all_to_all x1, blocking collectives, per_device(): lax.all_to_all(w_down, 'expert', split_axis=0, concat_axis=1, tiled=True)  29.5 us
    reduce_scatter x1, waiting for transfers between devices, per_device(): lax.psum_scatter(jnp.dot(mixed, tower_in, preferred_element_type=jnp.floa...  27.9 us
    all_to_all x1, blocking collectives, per_device(): lax.all_to_all(outgoing, 'expert', split_axis=0, concat_axis=0, tiled=True)  19.8 us
    all_gather x1, blocking collectives, per_device(): full_rows = lax.all_gather(requests, ('tensor', 'rep'), axis=1, tiled=True)  16.4 us
    unnamed x22, local copies, waits for them, and re-layouts  7.94 us
    dot_general x1, matrix products, per_device(): jnp.einsum('sech,edh->secd', hidden, serve_down, preferred_element_type=j...  5.47 us
  transfers between devices with their start and end apart: 3, of which 3 were waited for; matrix products, arithmetic and copies ran while one was open for 0% of the time, Pallas kernels for 0%

commit v1 on v0

--- a/solution.py
+++ b/solution.py
@@ -2,6 +2,17 @@
 import jax.numpy as jnp
 from jax import lax
 from jax.sharding import PartitionSpec as P
+
+
+def cut_along(x, dim, count):
+    before, after = (x.shape[:dim], x.shape[dim + 1 :])
+    return jnp.moveaxis(x.reshape(*before, count, -1, *after), dim, 0)
+
+
+def joined_along(parts, dim):
+    parts = jnp.moveaxis(parts, 0, dim)
+    lengths = parts.shape
+    return parts.reshape(*lengths[:dim], lengths[dim] * lengths[dim + 1], *lengths[dim + 2 :])
 
 
 def tower_head(pre, tower_bias, tower_out, out_bias):
@@ -34,7 +45,14 @@
     ).astype(jnp.bfloat16)
     full_rows = lax.all_gather(requests, ("tensor", "rep"), axis=1, tiled=True)
     outgoing = jnp.dot(spread, full_rows, preferred_element_type=jnp.float32).astype(jnp.bfloat16)
-    incoming = lax.all_to_all(outgoing, "expert", split_axis=0, concat_axis=0, tiled=True)
+    size, index = (lax.axis_size("expert"), lax.axis_index("expert"))
+    blocks = cut_along(outgoing, 0, size)
+    done = [blocks[index]]
+    for step in range(1, size):
+        sent = blocks[index ^ step]
+        done.append(lax.ppermute(sent, "expert", [(i, i ^ step) for i in range(size)]))
+    blocks = jnp.stack(done)[index ^ jnp.arange(size)]
+    incoming = joined_along(blocks, 0)
     shaped = incoming.reshape(groups, local_experts, capacity, incoming.shape[1])
     hidden_pre = jnp.einsum("secd,edh->sech", shaped, serve_up, preferred_element_type=jnp.float32)
     hidden = jax.nn.relu(hidden_pre).astype(jnp.bfloat16)

time: 199 us -> 177 us (0.89)
  blocking collectives: 95.8 us -> 15 us
  waiting for transfers between devices: 65.8 us -> 113 us
  starting transfers between devices: 3.68 us -> 17 us
    all_to_all x3 -> x0, blocking collectives: 79.4 us -> none  [the longest x1 30.1 us: per_device(): lax.all_to_all(w_up, 'expert', split_axis=0, concat_axis=1, tiled=True)]
    all_to_all x0 -> x2, waiting for transfers between devices: none -> 25.6 us  [the longest x1 25.6 us: per_device(): lax.all_to_all(w_up, 'expert', split_axis=0, concat_axis=1, tiled=True)]
    ppermute x0 -> x3, waiting for transfers between devices: none -> 20.4 us  [per_device(): lax.ppermute(sent, 'expert', [(i, i ^ step) for i in range(size)])]
    all_to_all x0 -> x2, starting transfers between devices: none -> 9.83 us  [the longest x1 5.34 us: per_device(): lax.all_to_all(w_up, 'expert', split_axis=0, concat_axis=1, tiled=True)]
    ppermute x0 -> x3, starting transfers between devices: none -> 3.55 us  [per_device(): lax.ppermute(sent, 'expert', [(i, i ^ step) for i in range(size)])]
    unnamed x22 -> x24, local copies, waits for them, and re-layouts: 7.94 us -> 7.09 us
  transfers between devices with their start and end apart: 3 -> 8, of which waited for: 3 -> 6; matrix products, arithmetic and copies ran while one was open for 0% -> 2% of each run, Pallas kernels for 0% -> 0%
where the time goes in v1:
time: 177 us
  waiting for transfers between devices  113 us (64%)
  starting transfers between devices  17 us (10%)
  blocking collectives  15 us (8%)
  between operations  14.2 us (8%)
  local copies, waits for them, and re-layouts  8.59 us (5%)
  matrix products  6.74 us (4%)
  other arithmetic  2.38 us (1%)
    unnamed x3, waiting for transfers between devices  33.6 us
    reduce_scatter x1, waiting for transfers between devices, per_device(): lax.psum_scatter(jnp.dot(mixed, tower_in, preferred_element_type=jnp.floa...  27.9 us
    all_to_all x1, waiting for transfers between devices, per_device(): lax.all_to_all(w_up, 'expert', split_axis=0, concat_axis=1, tiled=True)  25.6 us
    ppermute x3, waiting for transfers between devices, per_device(): lax.ppermute(sent, 'expert', [(i, i ^ step) for i in range(size)])  20.4 us
    all_gather x1, blocking collectives, per_device(): full_rows = lax.all_gather(requests, ('tensor', 'rep'), axis=1, tiled=True)  15 us
    unnamed x24, local copies, waits for them, and re-layouts  7.09 us
    all_to_all x1, starting transfers between devices, per_device(): lax.all_to_all(w_up, 'expert', split_axis=0, concat_axis=1, tiled=True)  5.34 us
    all_to_all x1, waiting for transfers between devices, per_device(): lax.all_to_all(expert_out, 'expert', split_axis=0, concat_axis=0, tiled=T...  5.18 us
  transfers between devices with their start and end apart: 8, of which 6 were waited for; matrix products, arithmetic and copies ran while one was open for 2% of the time, Pallas kernels for 0%

profile of v1, /device:TPU:0, one launch (start us, length us, event | category | flops | bytes accessed | tf_op | source)
XLA Modules:
  0.0 176.7 jit_solution(4703577674723129958)
XLA Ops:
  7.2 0.0 copy-start
  7.2 5.3 %all-to-all-start = ((bf16[4,384,768]{2,1,0:T(8,128)(2,1)}), bf16[4,384,768]{2,1,0:T(8,128)(2,1)S(1)}, u32[]{:S(2)}, u32[]{:S(2)}) async-start(bf16[4,384,768]{2,1,0:T(8,128)(2,1)} %param.12), calls=%async_computation | async-start | bytes 4718592 | tf_op jit(solution)/shard_map/all_to_all | solution.py:34
  12.5 0.1 copy.32
  12.6 0.1 eq.85
  12.8 0.1 eq.81
  12.9 1.2 reduce-window.6
  14.2 0.1 slice.28
  14.2 0.1 copy.34
  14.4 0.1 copy.35
  14.5 0.1 add_bitcast_fusion
  14.6 25.6 %all-to-all-done = bf16[4,384,768]{2,1,0:T(8,128)(2,1)S(1)} async-done(((bf16[4,384,768]{2,1,0:T(8,128)(2,1)}), bf16[4,384,768]{2,1,0:T(8,128)(2,1)S(1)}, u32[]{:S(2)}, u32[]{:S(2)}) %all-to-all-start) | async-done | bytes 2359328 | tf_op jit(solution)/shard_map/all_to_all | solution.py:34
  40.2 1.4 copy-done.1
  41.6 4.5 %all-to-all-start.1 = ((bf16[4,384,768]{2,1,0:T(8,128)(2,1)}), bf16[4,384,768]{2,1,0:T(8,128)(2,1)}, u32[]{:S(2)}, u32[]{:S(2)}) async-start(bf16[4,384,768]{2,1,0:T(8,128)(2,1)} %param.13), calls=%async_computation.1 | async-start | bytes 4718592 | tf_op jit(solution)/shard_map/all_to_all | solution.py:35
  46.1 0.0 reduce-scatter.7.cloned.1.call-start
  46.2 0.1 reduce_sum.21
  46.3 0.1 copy.36
  46.4 15.0 %all_gather.3 = bf16[128,1536]{0,1:T(8,128)(2,1)S(1)} all-gather(bf16[128,192]{0,1:T(8,128)(2,1)S(1)} %copy-done.3), channel_id=1, replica_groups=mesh['expert'=4,'tensor'=4,'rep'=2] {'tensor','rep'}, dimensions={1}, use_global_device_ids=true | all-gather | bytes 442368 | tf_op jit(solution)/shard_map/all_gather | solution.py:46
  61.4 0.5 convolution_convert_fusion
  61.9 0.1 constant_dynamic-slice_fusion
  61.9 2.9 %collective-permute-start.2 = (bf16[96,1536]{1,0:T(8,128)(2,1)S(1)}, bf16[96,1536]{1,0:T(8,128)(2,1)S(1)}, u32[]{:S(2)}, u32[]{:S(2)}) collective-permute-start(bf16[96,1536]{1,0:T(8,128)(2,1)S(1)} %get-tuple-element.7), channel_id=1, source_target_pairs={{0,24},{8,16},{16,8},{24,0},{1,25},{9,17},{17,9},{25,1},{2,26},{10... | collective-permute-start | bytes 884744 | tf_op jit(solution)/shard_map/ppermute | solution.py:53
  64.8 0.6 collective-permute-start
  65.4 0.1 collective-permute-start.1
  65.5 16.9 %collective-permute-done.2 = bf16[96,1536]{1,0:T(8,128)(2,1)S(1)} collective-permute-done((bf16[96,1536]{1,0:T(8,128)(2,1)S(1)}, bf16[96,1536]{1,0:T(8,128)(2,1)S(1)}, u32[]{:S(2)}, u32[]{:S(2)}) %collective-permute-start.2) | collective-permute-done | bytes 294944 | tf_op jit(solution)/shard_map/ppermute | solution.py:53
  82.4 3.6 %collective-permute-done = bf16[96,1536]{1,0:T(8,128)(2,1)S(1)} collective-permute-done((bf16[96,1536]{1,0:T(8,128)(2,1)S(1)}, bf16[96,1536]{1,0:T(8,128)(2,1)S(1)}, u32[]{:S(2)}, u32[]{:S(2)}) %collective-permute-start) | collective-permute-done | bytes 294944 | tf_op jit(solution)/shard_map/ppermute | solution.py:53
  86.0 0.0 collective-permute-done.1
  86.0 0.1 pad_maximum_fusion
  86.1 0.6 gather_fusion
  86.8 4.8 %fusion = bf16[4,1,96,1536]{3,2,0,1:T(8,128)(2,1)S(1)} fusion(bf16[1536,768,1]{1,0,2:T(8,128)(2,1)} %bitcast.16, bf16[4,96,1536]{2,1,0:T(8,128)(2,1)S(1)} %gather_fusion, bf16[1536,768,1]{1,0,2:T(8,128)(2,1)} %bitcast.68), kind=kOutput, calls=%fused_computation.3 | convolution fusion | flops 1813118976 | bytes 7077888 | tf_op jit(solution)/shard_map/sech,edh->secd/dot_general | solution.py:59
  91.6 1.1 copy.38
  92.6 1.9 %reshape.93 = bf16[1536,384]{1,0:T(8,128)(2,1)} reshape(bf16[1536,1,4,96]{3,2,1,0:T(4,128)(2,1)S(1)} %bitcast.66) | data formatting | bytes 2359296
  94.5 0.0 reduce-scatter.7.cloned.1.call-update
  94.6 0.0 copy-start.5
  94.6 33.6 %reduce-scatter.7.cloned.1.call-done = bf16[192,384]{1,0:T(8,128)(2,1)} async-done(((bf16[1536,384]{1,0:T(8,128)(2,1)}), bf16[192,384]{1,0:T(8,128)(2,1)}) %reduce-scatter.7.cloned.1.call-update) | async-done | bytes 147472
  128.2 1.1 reshape.94
  129.2 0.0 copy-start.6
  129.2 0.0 copy-start.8
  129.3 0.8 copy.39
  130.1 3.6 %all-to-all-start.2 = ((bf16[4,96,192]{2,1,0:T(8,128)(2,1)}), bf16[4,96,192]{2,1,0:T(8,128)(2,1)S(1)}, u32[]{:S(2)}, u32[]{:S(2)}) async-start(bf16[4,96,192]{2,1,0:T(8,128)(2,1)} %bitcast.20), calls=%async_computation.2 | async-start | bytes 393216 | tf_op jit(solution)/shard_map/all_to_all | solution.py:68
  133.7 5.2 %all-to-all-done.2 = bf16[4,96,192]{2,1,0:T(8,128)(2,1)S(1)} async-done(((bf16[4,96,192]{2,1,0:T(8,128)(2,1)}), bf16[4,96,192]{2,1,0:T(8,128)(2,1)S(1)}, u32[]{:S(2)}, u32[]{:S(2)}) %all-to-all-start.2) | async-done | bytes 147488 | tf_op jit(solution)/shard_map/all_to_all | solution.py:68
  138.9 0.3 convolution_multiply_fusion
  139.2 0.3 fusion.3
  139.5 0.0 copy-start.2
  139.5 0.9 convolution_convert_fusion.2
  140.4 0.0 reduce-scatter.5.cloned.1.call-update
  140.4 27.9 %reduce-scatter.5.cloned.1.call-done = bf16[16,768]{1,0:T(8,128)(2,1)} async-done(((bf16[128,768]{1,0:T(8,128)(2,1)}), bf16[16,768]{1,0:T(8,128)(2,1)}) %reduce-scatter.5.cloned.1.call-update) | async-done | bytes 24592 | tf_op jit(solution)/shard_map/reduce_scatter | solution.py:74
  168.3 0.7 add_maximum_fusion
  169.1 0.1 multiply_reduce_fusion
  169.2 0.7 copy.37
  (25 shorter events, 0.2 us)
Async XLA Ops:
  7.2 132.3 %copy-start = (bf16[192,768]{1,0:T(8,128)(2,1)S(1)}, bf16[192,768]{1,0:T(8,128)(2,1)}, u32[]{:S(2)}) copy-start(bf16[192,768]{1,0:T(8,128)(2,1)} %param.14) | copy-start | bytes 884740
  7.2 5.3 %copy-start.4 = (s32[128,2]{0,1:T(2,128)S(1)}, s32[128,2]{0,1:T(2,128)}, u32[]{:S(2)}) copy-start(s32[128,2]{0,1:T(2,128)} %param.10) | copy-start | bytes 3076
  7.2 33.0 %all-to-all-start = ((bf16[4,384,768]{2,1,0:T(8,128)(2,1)}), bf16[4,384,768]{2,1,0:T(8,128)(2,1)S(1)}, u32[]{:S(2)}, u32[]{:S(2)}) async-start(bf16[4,384,768]{2,1,0:T(8,128)(2,1)} %param.12), calls=%async_computation | async-start | bytes 4718592 | tf_op jit(solution)/shard_map/all_to_all | solution.py:34
  14.6 31.8 %copy-start.3 = (bf16[128,192]{0,1:T(8,128)(2,1)S(1)}, bf16[128,192]{0,1:T(8,128)(2,1)}, u32[]{:S(2)}) copy-start(bf16[128,192]{0,1:T(8,128)(2,1)} %param.9) | copy-start | bytes 147460
  40.2 1.4 copy-start.1
  41.6 45.1 %all-to-all-start.1 = ((bf16[4,384,768]{2,1,0:T(8,128)(2,1)}), bf16[4,384,768]{2,1,0:T(8,128)(2,1)}, u32[]{:S(2)}, u32[]{:S(2)}) async-start(bf16[4,384,768]{2,1,0:T(8,128)(2,1)} %param.13), calls=%async_computation.1 | async-start | bytes 4718592 | tf_op jit(solution)/shard_map/all_to_all | solution.py:35
  46.1 82.1 %reduce-scatter.7.cloned.1.call-start = ((), (), s32[]{:S(2)}) async-start(), calls=%async_computation.6 | async-start | bytes 1327104
  61.9 20.4 %collective-permute-start.2 = (bf16[96,1536]{1,0:T(8,128)(2,1)S(1)}, bf16[96,1536]{1,0:T(8,128)(2,1)S(1)}, u32[]{:S(2)}, u32[]{:S(2)}) collective-permute-start(bf16[96,1536]{1,0:T(8,128)(2,1)S(1)} %get-tuple-element.7), channel_id=1, source_target_pairs={{0,24},{8,16},{16,8},{24,0},{1,25},{9,17},{17,9},{25,1},{2,26},{10... | collective-permute-start | bytes 884744 | tf_op jit(solution)/shard_map/ppermute | solution.py:53
  64.8 21.1 %collective-permute-start = (bf16[96,1536]{1,0:T(8,128)(2,1)S(1)}, bf16[96,1536]{1,0:T(8,128)(2,1)S(1)}, u32[]{:S(2)}, u32[]{:S(2)}) collective-permute-start(bf16[96,1536]{1,0:T(8,128)(2,1)S(1)} %get-tuple-element.9), channel_id=1, source_target_pairs={{0,8},{8,0},{16,24},{24,16},{1,9},{9,1},{17,25},{25,17},{2,10},{10... | collective-permute-start | bytes 884744 | tf_op jit(solution)/shard_map/ppermute | solution.py:53
  65.4 20.6 %collective-permute-start.1 = (bf16[96,1536]{1,0:T(8,128)(2,1)S(1)}, bf16[96,1536]{1,0:T(8,128)(2,1)S(1)}, u32[]{:S(2)}, u32[]{:S(2)}) collective-permute-start(bf16[96,1536]{1,0:T(8,128)(2,1)S(1)} %get-tuple-element.8), channel_id=1, source_target_pairs={{0,16},{8,24},{16,0},{24,8},{1,17},{9,25},{17,1},{25,9},{2,18},{10... | collective-permute-start | bytes 884744 | tf_op jit(solution)/shard_map/ppermute | solution.py:53
  94.5 39.2 %copy-start.7 = (f32[128,2]{0,1:T(2,128)S(1)}, f32[128,2]{0,1:T(2,128)}, u32[]{:S(2)}) copy-start(f32[128,2]{0,1:T(2,128)} %param.11) | copy-start | bytes 3076
  94.6 73.7 %copy-start.5 = (f32[768]{0:T(1024)S(1)}, f32[768]{0:T(1024)}, u32[]{:S(2)}) copy-start(f32[768]{0:T(1024)} %param.15) | copy-start | bytes 9220
  129.2 39.9 %copy-start.6 = (f32[3,256]{1,0:T(4,128)S(1)}, f32[3,256]{1,0:T(4,128)}, u32[]{:S(2)}) copy-start(f32[3,256]{1,0:T(4,128)} %param.16) | copy-start | bytes 9220
  129.2 40.0 %copy-start.8 = (f32[3]{0:T(128)S(1)}, f32[3]{0:T(128)}, u32[]{:S(2)}) copy-start(f32[3]{0:T(128)} %param.17) | copy-start | bytes 40
  130.1 8.8 %all-to-all-start.2 = ((bf16[4,96,192]{2,1,0:T(8,128)(2,1)}), bf16[4,96,192]{2,1,0:T(8,128)(2,1)S(1)}, u32[]{:S(2)}, u32[]{:S(2)}) async-start(bf16[4,96,192]{2,1,0:T(8,128)(2,1)} %bitcast.20), calls=%async_computation.2 | async-start | bytes 393216 | tf_op jit(solution)/shard_map/all_to_all | solution.py:68
  133.7 34.6 %reduce-scatter.5.cloned.1.call-start = ((), (), s32[]{:S(2)}) async-start(), calls=%async_computation.5 | async-start | bytes 221184 | tf_op jit(solution)/shard_map/reduce_scatter | solution.py:74
  139.5 30.4 %copy-start.2 = (bf16[128,192]{0,1:T(8,128)(2,1)}, bf16[128,192]{0,1:T(8,128)(2,1)S(1)}, u32[]{:S(2)}) copy-start(bf16[128,192]{0,1:T(8,128)(2,1)S(1)} %fusion.3) | copy-start | bytes 147460
Sparse Core Ops, SparseCore 0:
  94.7 33.4 reduce-scatter.6
  140.6 27.7 reduce-scatter.4
